TPU v7x, 32 devices: a whole 2x2x4 slice. The times are simulated.
32 devices in a mesh: groups: 2 (over x), tensor: 16 (over z, y, core).
Axes of the slice: x: 2, y: 2, z: 4, core: 2. Of those that a mesh axis runs over, the one named last changes fastest.
Arguments:
- video_state: float32 [128, 4096], P(('groups', 'tensor')), parts along dimension 0, may hold values from -54 to 54
- audio_state: float32 [128, 2048], P(('groups', 'tensor')), parts along dimension 0, may hold values from -54 to 54
- video_modulation: float32 [12, 4096], P('groups'), parts along dimension 0, may hold values from -3 to 3
- audio_modulation: float32 [12, 2048], P('groups'), parts along dimension 0, may hold values from -3 to 3
- video_query: bfloat16 [4096, 2048], P(None, 'tensor'), may hold values from -0.09375 to 0.09375
- audio_keyval: bfloat16 [2048, 2, 2048], P(None, None, 'tensor'), may hold values from -0.125 to 0.125
- video_output: bfloat16 [2048, 4096], P('tensor'), may hold values from -0.125 to 0.125
- audio_query: bfloat16 [2048, 2048], P(None, 'tensor'), may hold values from -0.125 to 0.125
- video_keyval: bfloat16 [4096, 2, 2048], P(None, None, 'tensor'), may hold values from -0.09375 to 0.09375
- audio_output: bfloat16 [2048, 2048], P('tensor'), may hold values from -0.125 to 0.125
- video_expand: bfloat16 [4096, 16384], P(None, 'tensor'), may hold values from -0.09375 to 0.09375
- video_shrink: bfloat16 [16384, 4096], P('tensor'), may hold values from -0.046875 to 0.046875
- audio_expand: bfloat16 [2048, 8192], P(None, 'tensor'), may hold values from -0.125 to 0.125
- audio_shrink: bfloat16 [8192, 2048], P('tensor'), may hold values from -0.0625 to 0.0625
Outputs:
- video_next: float32 [128, 4096], P(('groups', 'tensor')), parts along dimension 0
- audio_next: float32 [128, 2048], P(('groups', 'tensor')), parts along dimension 0
There are 2 independent parts, one for each index of `groups`. A program takes and returns all parts, laid end to end along the dimension named above; an argument that names none is the same for every part. Nothing has to cross between parts.
All inputs are finite; a program needn't handle non-finite values.
Results may differ from a plain program's by a relative error of at most 0.0029.
Values may be sent and summed in bfloat16 or wider, within the bound.
A program may use at most 64 MiB of HBM per device.

v0:
```python
import jax
import jax.numpy as jnp
from jax import lax
from jax.sharding import PartitionSpec as P

HEAD_DIM = 64
epsilon = 1e-06


def partner(block, axis, distance):
    count = lax.axis_size(axis)
    route = []
    for low in range(count):
        high = low | 1 << distance
        if high != low and high < count:
            route += [(low, high), (high, low)]
    return lax.ppermute(block, axis, route)


def modulate(states, modulation, first):
    normed = states * lax.rsqrt(jnp.mean(states * states, axis=-1, keepdims=True) + epsilon)
    return (normed * (1.0 + modulation[first + 1]) + modulation[first]).astype(jnp.bfloat16)


def head_normalize(tensor):
    values = tensor.astype(jnp.float32)
    return (values * lax.rsqrt(jnp.mean(values * values, axis=-1, keepdims=True) + epsilon)).astype(
        jnp.bfloat16
    )


def softmax_weights(scores):
    expo = jnp.exp(scores)
    return (expo / jnp.sum(expo, axis=-1, keepdims=True)).astype(jnp.bfloat16)


def local_heads(queries, key_part, value_part):
    query_count, width = queries.shape
    source_count = key_part.shape[0]
    head_count = width // HEAD_DIM
    query_hat = head_normalize(queries.reshape(query_count, head_count, HEAD_DIM))
    key_hat = head_normalize(key_part.reshape(source_count, head_count, HEAD_DIM))
    scores = jnp.einsum(
        "qhd,khd->hqk", query_hat, key_hat, preferred_element_type=jnp.float32
    ) * HEAD_DIM ** (-0.5)
    weights = softmax_weights(scores)
    values = value_part.reshape(source_count, head_count, HEAD_DIM)
    mixed = jnp.einsum("hqk,khd->qhd", weights, values, preferred_element_type=jnp.float32)
    return mixed.astype(jnp.bfloat16).reshape(query_count, width)


def project_attend(query_rows, source_rows, query_weight, keyval_weight):
    width = query_weight.shape[1]
    queries = jnp.dot(query_rows, query_weight, preferred_element_type=jnp.float32).astype(
        jnp.bfloat16
    )
    flat_weight = keyval_weight.reshape(keyval_weight.shape[0], 2 * width)
    keyvals = jnp.dot(source_rows, flat_weight, preferred_element_type=jnp.float32).astype(
        jnp.bfloat16
    )
    key_part = keyvals[:, :width]
    value_part = keyvals[:, width:]
    if width >= HEAD_DIM:
        return local_heads(queries, key_part, value_part)
    query_float = queries.astype(jnp.float32)
    key_float = key_part.astype(jnp.float32)
    query_square = jnp.sum(query_float * query_float, axis=1, keepdims=True)
    key_square = jnp.sum(key_float * key_float, axis=1, keepdims=True)
    other_query, other_key = partner((query_square, key_square), "tensor", 0)
    query_hat = (query_float * lax.rsqrt((query_square + other_query) / HEAD_DIM + epsilon)).astype(
        jnp.bfloat16
    )
    key_hat = (key_float * lax.rsqrt((key_square + other_key) / HEAD_DIM + epsilon)).astype(
        jnp.bfloat16
    )
    partial_scores = jnp.einsum("qd,kd->qk", query_hat, key_hat, preferred_element_type=jnp.float32)
    other_scores = partner(partial_scores, "tensor", 0)
    scores = (partial_scores + other_scores) * HEAD_DIM ** (-0.5)
    weights = softmax_weights(scores)
    return jnp.dot(weights, value_part, preferred_element_type=jnp.float32).astype(jnp.bfloat16)


def output_rows(mixed, weight):
    return jnp.dot(mixed, weight, preferred_element_type=jnp.float32)


def feed_rows(inputs, expand, shrink):
    hidden = jnp.dot(inputs, expand, preferred_element_type=jnp.float32)
    hidden = jax.nn.gelu(hidden, approximate=True).astype(jnp.bfloat16)
    return jnp.dot(hidden, shrink, preferred_element_type=jnp.float32)


def on_device(
    video_state,
    audio_state,
    video_modulation,
    audio_modulation,
    video_query,
    audio_keyval,
    video_output,
    audio_query,
    video_keyval,
    audio_output,
    video_expand,
    video_shrink,
    audio_expand,
    audio_shrink,
):
    video_count = video_state.shape[0]
    audio_own = modulate(audio_state, audio_modulation, 0)
    video_whole = lax.all_gather(video_state, "tensor", axis=0, tiled=True)
    video_normed = modulate(video_whole, video_modulation, 0)
    audio_normed = lax.all_gather(audio_own, "tensor", axis=0, tiled=True)
    video_mixed = project_attend(video_normed, audio_normed, video_query, audio_keyval)
    audio_mixed = project_attend(audio_normed, video_normed, audio_query, video_keyval)
    audio_term = lax.psum_scatter(
        output_rows(audio_mixed, audio_output), "tensor", scatter_dimension=0, tiled=True
    )
    audio_mid = audio_state + audio_modulation[2] * audio_term
    audio_inner_own = modulate(audio_mid, audio_modulation, 3)
    partial_term = jnp.dot(video_mixed, video_output, preferred_element_type=jnp.float32)
    full_term = lax.psum(partial_term, "tensor")
    video_mid_whole = video_whole + video_modulation[2] * full_term
    video_inner = modulate(video_mid_whole, video_modulation, 3)
    first_row = lax.axis_index("tensor") * video_count
    video_mid = lax.dynamic_slice_in_dim(video_mid_whole, first_row, video_count, 0)
    audio_inner = lax.all_gather(audio_inner_own, "tensor", axis=0, tiled=True)
    video_feed = lax.psum_scatter(
        feed_rows(video_inner, video_expand, video_shrink),
        "tensor",
        scatter_dimension=0,
        tiled=True,
    )
    audio_feed = lax.psum_scatter(
        feed_rows(audio_inner, audio_expand, audio_shrink),
        "tensor",
        scatter_dimension=0,
        tiled=True,
    )
    video_next = video_mid + video_modulation[5] * video_feed
    audio_next = audio_mid + audio_modulation[5] * audio_feed
    return (video_next, audio_next)


def solution(mesh):
    placed = (
        P(("groups", "tensor"), None),
        P(("groups", "tensor"), None),
        P("groups", None),
        P("groups", None),
        P(None, "tensor"),
        P(None, None, "tensor"),
        P("tensor", None),
        P(None, "tensor"),
        P(None, None, "tensor"),
        P("tensor", None),
        P(None, "tensor"),
        P("tensor", None),
        P(None, "tensor"),
        P("tensor", None),
    )
    return jax.shard_map(
        on_device,
        mesh=mesh,
        in_specs=placed,
        out_specs=(P(("groups", "tensor"), None), P(("groups", "tensor"), None)),
        check_vma=False,
    )
```

profile of v0, /device:TPU:0, one launch (start us, length us, event | category | flops | bytes accessed | tf_op | source)
XLA Modules:
  0.0 302.8 jit_solution(14228679446785322309)
XLA Ops:
  8.0 1.8 fusion.80
  9.7 0.9 multiply_reduce_fusion.7
  10.6 0.8 fusion.54
  11.5 24.0 %all-gather.1 = bf16[16,4,2048]{2,1,0:T(4,128)(2,1)S(1)} all-gather(bf16[1,4,2048]{2,1,0:T(4,128)(2,1)S(1)} %fusion.54), channel_id=1, replica_groups=mesh['groups'=2,'tensor'=16] {'tensor'}, dimensions={0}, use_global_device_ids=true | all-gather | bytes 278528 | tf_op jit(solution)/shard_map/all_gather | solution.py:113
  35.5 1.3 fusion.9
  36.9 1.5 convolution_convert_fusion.2
  40.3 10.6 %all-gather.5.cloned.1.call-done = f32[16,4,4096]{2,1,0:T(4,128)} async-done(((f32[1,4,4096]{2,1,0:T(4,128)}), f32[16,4,4096]{2,1,0:T(4,128)}) %all-gather.5.cloned.1.call-update) | async-done | bytes 1048592 | tf_op jit(solution)/shard_map/all_gather | solution.py:111
  50.9 1.6 reshape.111
  52.7 2.1 fusion.5
  55.9 1.6 fusion.8
  58.1 0.9 convolution_convert_fusion
  59.0 2.1 fusion.84
  61.6 0.9 convolution_convert_fusion.1
  62.5 2.6 fusion.83
  66.4 93.9 %all-reduce.10.cloned.1.call-done = (f32[64,4096]{1,0:T(8,128)}, f32[64,2048]{1,0:T(8,128)}) async-done(((f32[64,4096]{1,0:T(8,128)}, f32[64,2048]{1,0:T(8,128)}), (f32[64,4096]{1,0:T(8,128)}, f32[64,2048]{1,0:T(8,128)})) %all-reduce.10.cloned.1.call-update) | async-done | bytes 1572880 | tf_op jit(solution)/shard_map/psum | solution.py:122
  160.3 1.0 multiply_reduce_fusion.6
  161.4 21.4 %all-gather.2 = bf16[16,4,2048]{2,1,0:T(4,128)(2,1)} all-gather(bf16[1,4,2048]{2,1,0:T(4,128)(2,1)S(1)} %fusion.55), channel_id=1, replica_groups=mesh['groups'=2,'tensor'=16] {'tensor'}, dimensions={0}, use_global_device_ids=true | all-gather | bytes 278528 | tf_op jit(solution)/shard_map/all_gather | solution.py:127
  182.8 1.0 reshape.115
  183.8 2.5 multiply_reduce_fusion
  186.4 3.4 %fusion.37 = f32[64,2048]{1,0:T(8,128)} fusion(bf16[512,2048]{1,0:T(8,128)(2,1)S(1)} %copy-done, bf16[64,2048]{1,0:T(8,128)(2,1)S(1)} %reshape.115, bf16[2048,512]{1,0:T(8,128)(2,1)} %param.26), kind=kOutput, calls=%fused_computation.49 | convolution fusion | flops 268730368 | bytes 4980736 | tf_op jit(solution)/shard_map/dot_general | solution.py:90
  189.8 9.9 %fusion.24 = f32[64,4096]{1,0:T(8,128)} fusion(bf16[1024,4096]{1,0:T(8,128)(2,1)} %param.25, bf16[4096,1024]{1,0:T(8,128)(2,1)} %param.24, f32[64,4096]{1,0:T(8,128)S(1)} %copy-done.1, f32[4096]{0:T(1024)S(1)} %bitcast.60, f32[4096]{0:T(1024)S(1)} %bitcast.61, f32[64]{0:T(128)S(1)} %add_rsqrt_fusion.5), kind=kOutput, calls=%fused_computation.35 | convolution fusion | flops 1075380224 | bytes 18907392 | tf_op jit(solution)/shard_map/dot_general | solution.py:90
  199.8 93.4 %all-reduce.8.cloned.1.call-done = (f32[64,4096]{1,0:T(8,128)}, f32[64,2048]{1,0:T(8,128)}) async-done(((f32[64,4096]{1,0:T(8,128)}, f32[64,2048]{1,0:T(8,128)}), (f32[64,4096]{1,0:T(8,128)}, f32[64,2048]{1,0:T(8,128)})) %all-reduce.8.cloned.1.call-update) | async-done | bytes 1572880
  293.2 1.5 fusion.44
  294.7 1.6 fusion.39
  (63 shorter events, 5.7 us)
Async XLA Ops:
  7.2 179.2 %copy-start = (bf16[512,2048]{1,0:T(8,128)(2,1)S(1)}, bf16[512,2048]{1,0:T(8,128)(2,1)}, u32[]{:S(2)}) copy-start(bf16[512,2048]{1,0:T(8,128)(2,1)} %param.27) | copy-start | bytes 6291460
  7.2 32.4 %copy-start.3 = (f32[6,4096]{1,0:T(8,128)S(1)}, f32[6,4096]{1,0:T(8,128)}, u32[]{:S(2)}) copy-start(f32[6,4096]{1,0:T(8,128)} %param.16) | copy-start | bytes 294916
  7.2 43.8 %all-gather.5.cloned.1.call-start = ((), (), s32[]{:S(2)}) async-start(), calls=%async_computation | async-start | bytes 1114112 | tf_op jit(solution)/shard_map/all_gather | solution.py:111
  7.9 152.4 %all-reduce.10.cloned.1.call-start = ((), (), s32[]{:S(2)}) async-start(), calls=%async_computation.2 | async-start | bytes 3145728 | tf_op jit(solution)/shard_map/psum | solution.py:122
  40.3 14.5 %copy-start.4 = (f32[1,4096]{1,0:T(1,128)}, f32[1,4096]{1,0:T(1,128)S(1)}, u32[]{:S(2)}) copy-start(f32[1,4096]{1,0:T(1,128)S(1)} %get-tuple-element.11) | copy-start | bytes 49156
  40.3 14.6 %copy-start.5 = (f32[1,4096]{1,0:T(1,128)}, f32[1,4096]{1,0:T(1,128)S(1)}, u32[]{:S(2)}) copy-start(f32[1,4096]{1,0:T(1,128)S(1)} %get-tuple-element.12) | copy-start | bytes 49156
  61.4 3.8 %copy-start.13 = (u32[32]{0:T(128)S(1)}, u32[32]{0:T(128)}, u32[]{:S(2)}) copy-start(u32[32]{0:T(128)} %constant.50) | copy-start | bytes 388
  61.4 99.0 %copy-start.2 = (f32[4,2048]{1,0:T(4,128)S(1)}, f32[4,2048]{1,0:T(4,128)}, u32[]{:S(2)}) copy-start(f32[4,2048]{1,0:T(4,128)} %param.15) | copy-start | bytes 98308
  61.4 98.9 %copy-start.12 = (f32[1,2048]{1,0:T(1,128)S(1)}, f32[1,2048]{1,0:T(1,128)}, u32[]{:S(2)}) copy-start(f32[1,2048]{1,0:T(1,128)} %get-tuple-element.17) | copy-start | bytes 24580
  61.5 99.8 %copy-start.10 = (f32[1,2048]{1,0:T(1,128)S(1)}, f32[1,2048]{1,0:T(1,128)}, u32[]{:S(2)}) copy-start(f32[1,2048]{1,0:T(1,128)} %get-tuple-element.20) | copy-start | bytes 24580
  61.6 99.8 %copy-start.11 = (f32[1,2048]{1,0:T(1,128)S(1)}, f32[1,2048]{1,0:T(1,128)}, u32[]{:S(2)}) copy-start(f32[1,2048]{1,0:T(1,128)} %get-tuple-element.21) | copy-start | bytes 24580
  65.1 228.1 %all-reduce.8.cloned.1.call-start = ((), (), s32[]{:S(2)}) async-start(), calls=%async_computation.1 | async-start | bytes 3145728
  186.3 3.4 %copy-start.1 = (f32[64,4096]{1,0:T(8,128)S(1)}, f32[64,4096]{1,0:T(8,128)}, u32[]{:S(2)}) copy-start(f32[64,4096]{1,0:T(8,128)} %get-tuple-element.9) | copy-start | bytes 3145732
  186.3 3.4 %copy-start.7 = (f32[1,4096]{1,0:T(1,128)S(1)}, f32[1,4096]{1,0:T(1,128)}, u32[]{:S(2)}) copy-start(f32[1,4096]{1,0:T(1,128)} %get-tuple-element.14) | copy-start | bytes 49156
  186.3 3.4 %copy-start.8 = (f32[1,4096]{1,0:T(1,128)S(1)}, f32[1,4096]{1,0:T(1,128)}, u32[]{:S(2)}) copy-start(f32[1,4096]{1,0:T(1,128)} %get-tuple-element.15) | copy-start | bytes 49156
  189.8 103.4 %copy-start.9 = (f32[1,2048]{1,0:T(1,128)S(1)}, f32[1,2048]{1,0:T(1,128)}, u32[]{:S(2)}) copy-start(f32[1,2048]{1,0:T(1,128)} %get-tuple-element.16) | copy-start | bytes 24580
  189.8 104.9 %copy-start.6 = (f32[1,4096]{1,0:T(1,128)S(1)}, f32[1,4096]{1,0:T(1,128)}, u32[]{:S(2)}) copy-start(f32[1,4096]{1,0:T(1,128)} %get-tuple-element.10) | copy-start | bytes 49156
Sparse Core Ops, SparseCore 0:
  10.2 40.7 all-gather.4
  65.2 95.0 all-reduce.9
  199.9 93.2 all-reduce.7
where the time goes:
time: 304 us; the launch traced here: 303 us
  waiting for transfers between devices  199 us (65%)
  blocking collectives  45.4 us (15%)
  matrix products  26.7 us (9%)
  between operations  14.8 us (5%)
  other arithmetic  12 us (4%)
  local copies, waits for them, and re-layouts  5.14 us (2%)
    unnamed x4, waiting for transfers between devices  94.1 us
    psum x1, waiting for transfers between devices, on_device(): full_term = lax.psum(partial_term, 'tensor')  93.9 us
    all_gather x1, blocking collectives, on_device(): audio_normed = lax.all_gather(audio_own, 'tensor', axis=0, tiled=True)  24 us
    all_gather x1, blocking collectives, on_device(): audio_inner = lax.all_gather(audio_inner_own, 'tensor', axis=0, tiled=True)  21.4 us
    dot_general x2, matrix products, feed_rows(): return jnp.dot(hidden, shrink, preferred_element_type=jnp.float32)  13.4 us
    all_gather x1, waiting for transfers between devices, on_device(): video_whole = lax.all_gather(video_state, 'tensor', axis=0, tiled=True)  10.6 us
  transfers between devices with their start and end apart: 3, of which 3 were waited for; matrix products, arithmetic and copies ran while one was open for 3% of the time, Pallas kernels for 0%

commit v1 on v0

--- a/solution.py
+++ b/solution.py
@@ -2,6 +2,7 @@
 import jax.numpy as jnp
 from jax import lax
 from jax.sharding import PartitionSpec as P
+from jax.lax import all_gather
 
 HEAD_DIM = 64
 epsilon = 1e-06
@@ -119,7 +120,11 @@
     audio_mid = audio_state + audio_modulation[2] * audio_term
     audio_inner_own = modulate(audio_mid, audio_modulation, 3)
     partial_term = jnp.dot(video_mixed, video_output, preferred_element_type=jnp.float32)
-    full_term = lax.psum(partial_term, "tensor")
+
+    def plan_pieces_all(inner_x, axis_key):
+        return all_gather(inner_x, axis_key).sum(axis=0)
+
+    full_term = plan_pieces_all(partial_term, "tensor")
     video_mid_whole = video_whole + video_modulation[2] * full_term
     video_inner = modulate(video_mid_whole, video_modulation, 3)
     first_row = lax.axis_index("tensor") * video_count

time: 304 us -> 406 us (1.34)
  waiting for transfers between devices: 199 us -> 292 us
  other arithmetic: 12 us -> 19.9 us
    all_gather x0 -> x1, waiting for transfers between devices: none -> 100 us  [plan_pieces_all(): return all_gather(inner_x, axis_key).sum(axis=0)]
    psum x1 -> x0, waiting for transfers between devices: 93.9 us -> none  [on_device(): full_term = lax.psum(partial_term, 'tensor')]
    unnamed x4 -> x6, waiting for transfers between devices: 94.1 us -> 181 us
    reduce_sum x0 -> x1, other arithmetic: none -> 7.88 us  [plan_pieces_all(): return all_gather(inner_x, axis_key).sum(axis=0)]
  transfers between devices with their start and end apart: 3 -> 4, of which waited for: 3 -> 4; matrix products, arithmetic and copies ran while one was open for 3% -> 4% of each run, Pallas kernels for 0% -> 0%
where the time goes in v1:
time: 406 us
  waiting for transfers between devices  292 us (72%)
  blocking collectives  48.1 us (12%)
  matrix products  25.1 us (6%)
  other arithmetic  19.9 us (5%)
  between operations  14.8 us (4%)
  local copies, waits for them, and re-layouts  5.14 us (1%)
    unnamed x6, waiting for transfers between devices  181 us
    all_gather x1, waiting for transfers between devices, plan_pieces_all(): return all_gather(inner_x, axis_key).sum(axis=0)  100 us
    all_gather x1, blocking collectives, on_device(): audio_inner = lax.all_gather(audio_inner_own, 'tensor', axis=0, tiled=True)  24.1 us
    all_gather x1, blocking collectives, on_device(): audio_normed = lax.all_gather(audio_own, 'tensor', axis=0, tiled=True)  24 us
    dot_general x2, matrix products, feed_rows(): return jnp.dot(hidden, shrink, preferred_element_type=jnp.float32)  13.6 us
    all_gather x1, waiting for transfers between devices, on_device(): video_whole = lax.all_gather(video_state, 'tensor', axis=0, tiled=True)  11.6 us
  transfers between devices with their start and end apart: 4, of which 4 were waited for; matrix products, arithmetic and copies ran while one was open for 4% of the time, Pallas kernels for 0%

profile of v1, /device:TPU:0, one launch (start us, length us, event | category | flops | bytes accessed | tf_op | source)
XLA Modules:
  0.0 405.7 jit_solution(4449643512973796201)
XLA Ops:
  8.0 1.8 fusion.80
  9.7 0.9 multiply_reduce_fusion.7
  10.6 0.8 fusion.54
  11.5 24.0 %all-gather.2 = bf16[16,4,2048]{2,1,0:T(4,128)(2,1)S(1)} all-gather(bf16[1,4,2048]{2,1,0:T(4,128)(2,1)S(1)} %fusion.54), channel_id=1, replica_groups=mesh['groups'=2,'tensor'=16] {'tensor'}, dimensions={0}, use_global_device_ids=true | all-gather | bytes 278528 | tf_op jit(solution)/shard_map/all_gather | solution.py:114
  35.5 1.6 convolution_convert_fusion.2
  39.3 11.6 %all-gather.9.cloned.1.call-done = f32[16,4,4096]{2,1,0:T(4,128)} async-done(((f32[1,4,4096]{2,1,0:T(4,128)}), f32[16,4,4096]{2,1,0:T(4,128)}) %all-gather.9.cloned.1.call-update) | async-done | bytes 1048592 | tf_op jit(solution)/shard_map/all_gather | solution.py:112
  50.9 1.6 reshape.112
  52.7 1.6 fusion.8
  54.6 2.1 fusion.5
  58.1 0.9 convolution_convert_fusion
  59.0 2.1 fusion.84
  61.7 2.6 fusion.83
  65.6 85.5 %all-reduce.7.cloned.1.call-done = f32[64,2048]{1,0:T(8,128)} async-done(((f32[64,2048]{1,0:T(8,128)}), f32[64,2048]{1,0:T(8,128)}) %all-reduce.7.cloned.1.call-update) | async-done | bytes 524304
  151.2 1.0 multiply_reduce_fusion.6
  152.2 24.1 %all-gather.3 = bf16[16,4,2048]{2,1,0:T(4,128)(2,1)} all-gather(bf16[1,4,2048]{2,1,0:T(4,128)(2,1)S(1)} %fusion.55), channel_id=1, replica_groups=mesh['groups'=2,'tensor'=16] {'tensor'}, dimensions={0}, use_global_device_ids=true | all-gather | bytes 278528 | tf_op jit(solution)/shard_map/all_gather | solution.py:132
  176.3 1.0 reshape.116
  177.4 3.4 fusion.37
  180.7 100.1 %all-gather.7.cloned.1.call-done = f32[1024,4096]{1,0:T(8,128)} async-done(((f32[64,4096]{1,0:T(8,128)}), f32[1024,4096]{1,0:T(8,128)}) %all-gather.7.cloned.1.call-update) | async-done | bytes 16777232 | tf_op jit(solution)/shard_map/all_gather | solution.py:125
  280.9 7.9 %reduce_sum.104 = f32[64,4096]{1,0:T(8,128)} reduce(f32[16,64,4096]{2,1,0:T(8,128)} %bitcast.54, f32[]{:T(128)} %constant.14.clone.1), dimensions={0}, to_apply=%region_5.0 | reduce | flops 3932160 | bytes 17825796 | tf_op jit(solution)/shard_map/reduce_sum | solution.py:125
  288.7 2.5 multiply_reduce_fusion
  291.3 10.2 %fusion.24 = f32[64,4096]{1,0:T(8,128)} fusion(bf16[1024,4096]{1,0:T(8,128)(2,1)} %param.25, bf16[4096,1024]{1,0:T(8,128)(2,1)} %param.24, f32[64,4096]{1,0:T(8,128)} %get-tuple-element.7, f32[4096]{0:T(1024)S(1)} %bitcast.62, f32[4096]{0:T(1024)S(1)} %bitcast.63, f32[64]{0:T(128)S(1)} %add_rsqrt_fusion.5), kind=kOutput, calls=%fused_computation.35 | convolution fusion | flops 1075380224 | bytes 18907392 | tf_op jit(solution)/shard_map/dot_general | solution.py:91
  301.6 94.5 %all-reduce.9.cloned.1.call-done = (f32[64,4096]{1,0:T(8,128)}, f32[64,2048]{1,0:T(8,128)}) async-done(((f32[64,4096]{1,0:T(8,128)}, f32[64,2048]{1,0:T(8,128)}), (f32[64,4096]{1,0:T(8,128)}, f32[64,2048]{1,0:T(8,128)})) %all-reduce.9.cloned.1.call-update) | async-done | bytes 1572880
  396.0 1.5 fusion.44
  397.5 1.6 fusion.39
  (65 shorter events, 6.1 us)
Async XLA Ops:
  7.2 170.2 %copy-start = (bf16[512,2048]{1,0:T(8,128)(2,1)S(1)}, bf16[512,2048]{1,0:T(8,128)(2,1)}, u32[]{:S(2)}) copy-start(bf16[512,2048]{1,0:T(8,128)(2,1)} %param.27) | copy-start | bytes 6291460
  7.2 30.8 %copy-start.1 = (bf16[2048,128]{1,0:T(8,128)(2,1)S(1)}, bf16[2048,128]{1,0:T(8,128)(2,1)}, u32[]{:S(2)}) copy-start(bf16[2048,128]{1,0:T(8,128)(2,1)} %param.21) | copy-start | bytes 1572868
  7.2 43.8 %all-gather.9.cloned.1.call-start = ((), (), s32[]{:S(2)}) async-start(), calls=%async_computation.1 | async-start | bytes 1114112 | tf_op jit(solution)/shard_map/all_gather | solution.py:112
  7.9 143.2 %all-reduce.7.cloned.1.call-start = ((), (), s32[]{:S(2)}) async-start(), calls=%async_computation.2 | async-start | bytes 1048576
  35.5 3.1 copy-start.3
  57.9 3.7 copy-start.7
  61.1 3.3 copy-start.12
  61.1 90.0 %copy-start.2 = (f32[4,2048]{1,0:T(4,128)S(1)}, f32[4,2048]{1,0:T(4,128)}, u32[]{:S(2)}) copy-start(f32[4,2048]{1,0:T(4,128)} %param.15) | copy-start | bytes 98308
  61.1 90.0 %copy-start.11 = (f32[1,2048]{1,0:T(1,128)S(1)}, f32[1,2048]{1,0:T(1,128)}, u32[]{:S(2)}) copy-start(f32[1,2048]{1,0:T(1,128)} %get-tuple-element.15) | copy-start | bytes 24580
  61.2 91.0 %copy-start.9 = (f32[1,2048]{1,0:T(1,128)S(1)}, f32[1,2048]{1,0:T(1,128)}, u32[]{:S(2)}) copy-start(f32[1,2048]{1,0:T(1,128)} %get-tuple-element.18) | copy-start | bytes 24580
  61.2 91.0 %copy-start.10 = (f32[1,2048]{1,0:T(1,128)S(1)}, f32[1,2048]{1,0:T(1,128)}, u32[]{:S(2)}) copy-start(f32[1,2048]{1,0:T(1,128)} %get-tuple-element.19) | copy-start | bytes 24580
  61.2 219.7 %all-gather.7.cloned.1.call-start = ((), (), s32[]{:S(2)}) async-start(), calls=%async_computation | async-start | bytes 17825792 | tf_op jit(solution)/shard_map/all_gather | solution.py:125
  64.3 331.7 %all-reduce.9.cloned.1.call-start = ((), (), s32[]{:S(2)}) async-start(), calls=%async_computation.3 | async-start | bytes 3145728
  288.7 2.5 copy-start.5
  288.7 2.5 copy-start.6
  291.3 104.8 %copy-start.8 = (f32[1,2048]{1,0:T(1,128)S(1)}, f32[1,2048]{1,0:T(1,128)}, u32[]{:S(2)}) copy-start(f32[1,2048]{1,0:T(1,128)} %get-tuple-element.14) | copy-start | bytes 24580
  291.3 106.2 %copy-start.4 = (f32[1,4096]{1,0:T(1,128)S(1)}, f32[1,4096]{1,0:T(1,128)}, u32[]{:S(2)}) copy-start(f32[1,4096]{1,0:T(1,128)} %get-tuple-element.8) | copy-start | bytes 49156
Sparse Core Ops, SparseCore 0:
  10.2 40.7 all-gather.8
  61.3 89.8 all-reduce.6
  153.3 127.4 all-gather.6
  301.7 94.3 all-reduce.8
